TPU v7x, 32 devices: a whole 2x2x4 slice. The times are simulated.
32 devices in a mesh: lat: 4 (over y, x), ord: 4 (over z), batch: 2 (over core).
Axes of the slice: x: 2, y: 2, z: 4, core: 2. Of those that a mesh axis runs over, the one named last changes fastest.
Arguments:
- state_field: bfloat16 [512, 720, 1440], P(('batch', 'ord'), 'lat'), parts along dimension 0, may hold values from -6 to 6
- slot_order: int32 [512], replicated, may hold values from 0 to 511, each once
- legendre: bfloat16 [512, 720, 720], P(('lat', 'ord')), may hold values from -0.21875 to 0.21875
- degree_gain: float32 [720, 256], replicated, may hold values from 0.25 to 1.75
- mixing: bfloat16 [256, 256], replicated, may hold values from -0.375 to 0.375
Outputs:
- updated: bfloat16 [512, 720, 1440], P(('batch', 'ord'), 'lat'), parts along dimension 0
There are 2 independent parts, one for each index of `batch`. A program takes and returns all parts, laid end to end along the dimension named above; an argument that names none is the same for every part. Nothing has to cross between parts.
Inputs may be any that keep to these rules, and one draw needn't show every extreme that they name: `slot_order`: each of 0 to 511 stands once.
All inputs are finite; a program needn't handle non-finite values.
Results may differ from a plain program's by a relative error of at most 0.0054.
Values may be sent and summed in bfloat16 or wider, within the bound.
No kernel may reach another device: no remote copies, remote signals or barrier semaphores. Data moves between devices by JAX's collectives and lax.ppermute only.
A program may use at most 320 MiB of HBM per device.

v0:
```python
import math

import jax
import jax.numpy as jnp
from jax import lax
from jax.sharding import PartitionSpec as P


def tables(orders, lon_count):
    longitude = jnp.arange(lon_count, dtype=jnp.int32)
    phase = orders[:, None] * longitude[None, :] % lon_count
    angle = phase.astype(jnp.float32) * (2.0 * math.pi / lon_count)
    root = 1.0 / math.sqrt(lon_count)
    cosine = jnp.cos(angle)
    sine = jnp.sin(angle)
    forward = jnp.stack([cosine * root, -sine * root], axis=1).astype(jnp.bfloat16)
    weights = jnp.where(orders == 0, 1.0, 2.0).astype(jnp.float32) * root
    inverse = jnp.stack([cosine * weights[:, None], -sine * weights[:, None]], axis=1).astype(
        jnp.bfloat16
    )
    return (forward, inverse)


def shards(state_field, slot_order, legendre, degree_gain, mixing):
    channels, lat_rows, lon_count = state_field.shape
    all_slots = slot_order.shape[0]
    my_slots, degrees, latitudes = legendre.shape
    width = mixing.shape[0]
    lat_count = lax.axis_size("lat")
    ord_count = lax.axis_size("ord")
    forward, inverse = tables(slot_order, lon_count)
    fourier = lax.dot_general(
        forward.reshape(2 * all_slots, lon_count),
        state_field.reshape(channels * lat_rows, lon_count),
        (((1,), (1,)), ((), ())),
        preferred_element_type=jnp.float32,
    )
    fourier = fourier.astype(jnp.bfloat16)
    arrived = lax.all_to_all(
        fourier.reshape(1, all_slots, 2, channels, lat_rows),
        ("lat", "ord"),
        split_axis=1,
        concat_axis=0,
        tiled=True,
    )
    arrived = arrived.reshape(lat_count, ord_count, my_slots, 2, channels, lat_rows).transpose(
        2, 3, 1, 4, 0, 5
    )
    gathered = arrived.reshape(my_slots, 2 * width, latitudes)
    orders_here = lax.dynamic_slice_in_dim(
        slot_order, lax.axis_index(("lat", "ord")) * my_slots, my_slots, 0
    )
    padded_gain = jnp.concatenate([degree_gain, jnp.zeros((degrees, width), jnp.float32)], axis=0)
    spec = jnp.einsum("sjl,sxl->sjx", legendre, gathered, preferred_element_type=jnp.float32)

    def pick_rows(order_value):
        return lax.dynamic_slice_in_dim(padded_gain, order_value, degrees, 0)

    gain_rows = jax.vmap(pick_rows)(orders_here)
    kept = jnp.arange(degrees, dtype=jnp.int32)[None, :] < (degrees - orders_here)[:, None]
    filtered = jnp.where(
        kept[:, :, None, None],
        spec.reshape(my_slots, degrees, 2, width) * gain_rows[:, :, None, :],
        0.0,
    )
    filtered = filtered.astype(jnp.bfloat16)
    mixed = jnp.dot(
        filtered.reshape(my_slots * degrees * 2, width), mixing, preferred_element_type=jnp.float32
    )
    mixed = mixed.astype(jnp.bfloat16).reshape(my_slots, degrees, 2 * width)
    synth = jnp.einsum("sjx,sjl->sxl", mixed, legendre, preferred_element_type=jnp.float32).astype(
        jnp.bfloat16
    )
    outgoing = synth.reshape(my_slots, 2, ord_count, channels, lat_count, lat_rows).transpose(
        4, 2, 0, 1, 3, 5
    )
    outgoing = outgoing.reshape(lat_count * ord_count, my_slots, 2, channels, lat_rows)
    returned = lax.all_to_all(outgoing, ("lat", "ord"), split_axis=0, concat_axis=0, tiled=True)
    returned = returned.reshape(2 * all_slots, channels * lat_rows)
    back = lax.dot_general(
        returned,
        inverse.reshape(2 * all_slots, lon_count),
        (((0,), (0,)), ((), ())),
        preferred_element_type=jnp.float32,
    )
    back = back.reshape(channels, lat_rows, lon_count)
    return (state_field.astype(jnp.float32) + jax.nn.gelu(back, approximate=True)).astype(
        jnp.bfloat16
    )


def solution(mesh):
    placed = (P(("batch", "ord"), "lat", None), P(), P(("lat", "ord"), None, None), P(), P())
    return jax.shard_map(
        shards,
        mesh=mesh,
        in_specs=placed,
        out_specs=P(("batch", "ord"), "lat", None),
        check_vma=False,
    )
```

profile of v0, /device:TPU:0, one launch (start us, length us, event | category | flops | bytes accessed | tf_op | source)
XLA Modules:
  0.0 2427.6 jit_solution(18168118739355333888)
XLA Ops:
  0.7 14.0 multiply_convert_fusion.1
  14.7 2.9 pad_maximum_fusion
  17.7 7.4 copy.31
  25.1 3.6 convert_element_type.65
  28.7 24.3 %copy.32 = bf16[64,180,1440]{2,1,0:T(8,128)(2,1)} copy(bf16[64,180,1440]{2,0,1:T(8,128)(2,1)} %param.5) | data formatting | bytes 66355200 | tf_op args[0]
  53.0 41.1 %reshape.240 = bf16[11520,1440]{1,0:T(8,128)(2,1)} reshape(bf16[64,180,1440]{2,1,0:T(8,128)(2,1)} %copy.32) | data formatting | bytes 66355200 | tf_op jit(solution)/shard_map/reshape | solution.py:34
  94.1 42.8 %convolution_convert_fusion.1 = bf16[1024,11520]{1,0:T(8,128)(2,1)} fusion(bf16[1024,1440]{1,0:T(8,128)(2,1)S(1)} %copy-done.3, bf16[11520,1440]{1,0:T(8,128)(2,1)} %reshape.240), kind=kOutput, calls=%fused_computation.17 | convolution fusion | flops 33985658880 | bytes 59719680 | tf_op jit(solution)/shard_map/dot_general | solution.py:32
  136.9 105.4 %reshape.241 = bf16[1,512,2,64,180]{4,3,2,1,0:T(8,128)(2,1)} reshape(bf16[1024,11520]{1,0:T(8,128)(2,1)} %convolution_convert_fusion.1) | data formatting | bytes 47185920 | tf_op jit(solution)/shard_map/reshape | solution.py:40
  242.3 8.5 all-to-all-start
  251.7 66.9 %while.1 = (s32[]{:T(128)}, f32[1440,256]{1,0:T(8,128)S(1)}, s32[32,2]{0,1:T(2,128)S(1)}, f32[32,720,256]{2,1,0:T(8,128)}, s32[]{:T(128)}) while((s32[]{:T(128)}, f32[1440,256]{1,0:T(8,128)S(1)}, s32[32,2]{0,1:T(2,128)S(1)}, f32[32,720,256]{2,1,0:T(8,128)}, s32[]{:T(128)}) %tuple.21), condition=%wide.while_cond, body=%wide.while_body.sunk | while | flops 2 | bytes 1475173 | solution.py:57
  256.5 1.5 bitcast_dynamic-update-slice_fusion.2
  258.6 1.5 bitcast_dynamic-update-slice_fusion.2
  260.7 1.5 bitcast_dynamic-update-slice_fusion.2
  266.9 1.5 bitcast_dynamic-update-slice_fusion.2
  269.0 1.5 bitcast_dynamic-update-slice_fusion.2
  275.3 1.5 bitcast_dynamic-update-slice_fusion.2
  277.4 1.5 bitcast_dynamic-update-slice_fusion.2
  285.7 1.5 bitcast_dynamic-update-slice_fusion.2
  287.8 1.6 bitcast_dynamic-update-slice_fusion.2
  296.2 1.5 bitcast_dynamic-update-slice_fusion.2
  302.5 1.5 bitcast_dynamic-update-slice_fusion.2
  306.6 1.5 bitcast_dynamic-update-slice_fusion.2
  308.7 1.5 bitcast_dynamic-update-slice_fusion.2
  315.0 1.5 bitcast_dynamic-update-slice_fusion.2
  318.6 24.6 %mul.158 = f32[32,720,2,256]{3,2,1,0:T(2,128)} broadcast(f32[32,720,256]{2,1,0:T(8,128)} %get-tuple-element.12), dimensions={0,1,3} | broadcast | bytes 70778880 | tf_op jit(solution)/shard_map/mul | solution.py:63
  343.2 55.6 %mul.159 = f32[46080,256]{1,0:T(8,128)} reshape(f32[32,720,2,256]{3,2,1,0:T(2,128)} %mul.158) | data formatting | bytes 94371840 | tf_op jit(solution)/shard_map/mul | solution.py:63
  398.8 4.6 broadcast_in_dim.37
  403.4 12.5 broadcast_in_dim.38
  415.9 600.0 %all-to-all-done = bf16[1,512,2,64,180]{4,3,2,0,1:T(8,128)(2,1)} async-done(((bf16[1,512,2,64,180]{4,3,2,0,1:T(8,128)(2,1)}), bf16[1,512,2,64,180]{4,3,2,0,1:T(8,128)(2,1)}, u32[]{:S(2)}, u32[]{:S(2)}) %all-to-all-start) | async-done | bytes 23592992 | tf_op jit(solution)/shard_map/all_to_all | solution.py:39
  1015.9 48.2 %copy.53 = bf16[4,4,32,2,64,180]{5,0,4,1,3,2:T(4,128)(2,1)} copy(bf16[4,4,32,2,64,180]{5,4,3,2,1,0:T(8,128)(2,1)} %bitcast.1) | data formatting | bytes 47185920 | tf_op jit(solution)/shard_map/reshape | solution.py:46
  1064.1 57.0 %reshape.243 = bf16[32,512,720]{2,1,0:T(8,128)(2,1)} reshape(bf16[32,2,4,64,4,180]{5,4,3,2,1,0:T(4,128)(2,1)} %bitcast.34) | data formatting | bytes 47185920 | tf_op jit(solution)/shard_map/reshape | solution.py:49
  1121.1 40.9 %convolution_bitcast_fusion = f32[32,720,512]{2,1,0:T(8,128)} fusion(bf16[32,512,720]{2,1,0:T(8,128)(2,1)} %reshape.243, bf16[32,720,720]{2,1,0:T(8,128)(2,1)} %param.7), kind=kOutput, calls=%fused_computation.18 | convolution fusion | flops 16986931200 | bytes 103956480 | tf_op jit(solution)/shard_map/sjl,sxl->sjx/dot_general | solution.py:54
  1162.0 50.8 %reshape.244 = f32[46080,256]{1,0:T(8,128)} reshape(f32[32,720,512]{2,1,0:T(8,128)} %convolution_bitcast_fusion) | data formatting | bytes 94371840 | tf_op jit(solution)/shard_map/reshape | solution.py:63
  1212.8 40.1 %convolution_convert_fusion = bf16[46080,256]{1,0:T(8,128)(2,1)} fusion(bf16[256,256]{1,0:T(8,128)(2,1)S(1)} %copy-done, f32[46080,256]{1,0:T(8,128)} %reshape.244, f32[46080,256]{1,0:T(8,128)} %mul.159, pred[46080]{0:T(1024)(128)(4,1)S(1)} %broadcast_in_dim.38), kind=kOutput, calls=%fused_computation.12 | convolution fusion | flops 6086983680 | bytes 118141952 | tf_op jit(solution)/shard_map/dot_general | solution.py:67
  1252.9 34.0 %reshape.245 = bf16[32,720,512]{2,1,0:T(8,128)(2,1)} reshape(bf16[46080,256]{1,0:T(8,128)(2,1)} %convolution_convert_fusion) | data formatting | bytes 47185920 | tf_op jit(solution)/shard_map/reshape | solution.py:70
  1286.9 40.2 %convolution_convert_fusion.2 = bf16[32,512,720]{1,2,0:T(8,128)(2,1)} fusion(bf16[32,720,512]{2,1,0:T(8,128)(2,1)} %reshape.245, bf16[32,720,720]{2,1,0:T(8,128)(2,1)} %param.7), kind=kOutput, calls=%fused_computation.19 | convolution fusion | flops 16998727680 | bytes 80363520 | tf_op jit(solution)/shard_map/sjx,sjl->sxl/dot_general | solution.py:71
  1327.1 30.1 %copy.37 = bf16[32,512,720]{2,1,0:T(8,128)(2,1)} copy(bf16[32,512,720]{1,2,0:T(8,128)(2,1)} %convolution_convert_fusion.2) | data formatting | bytes 47185920 | tf_op jit(solution)/shard_map/convert_element_type | solution.py:71
  1357.2 67.0 %reshape.246 = bf16[32,2,4,64,4,180]{5,4,3,2,1,0:T(4,128)(2,1)} reshape(bf16[32,512,720]{2,1,0:T(8,128)(2,1)} %copy.37) | data formatting | bytes 47185920 | tf_op jit(solution)/shard_map/reshape | solution.py:74
  1424.2 23.0 copy.38
  1447.2 6.1 all-to-all-start.1
  1453.3 7.4 copy.40
  1460.8 3.6 convert_element_type.70
  1464.3 755.5 %all-to-all-done.1 = bf16[16,32,2,64,180]{4,3,2,1,0:T(8,128)(2,1)} async-done(((bf16[16,32,2,64,180]{4,3,2,1,0:T(8,128)(2,1)}), bf16[16,32,2,64,180]{4,3,2,1,0:T(8,128)(2,1)}, u32[]{:S(2)}, u32[]{:S(2)}) %all-to-all-start.1) | async-done | bytes 23592992 | tf_op jit(solution)/shard_map/all_to_all | solution.py:78
  2219.9 52.2 %reshape.248 = bf16[1024,11520]{1,0:T(8,128)(2,1)} reshape(bf16[16,32,2,64,180]{4,3,2,1,0:T(8,128)(2,1)} %all-to-all-done.1) | data formatting | bytes 47185920 | tf_op jit(solution)/shard_map/reshape | solution.py:79
  2272.0 30.5 %copy.39 = bf16[11520,1024]{1,0:T(8,128)(2,1)} copy(bf16[11520,1024]{0,1:T(8,128)(2,1)} %bitcast.37) | data formatting | bytes 47185920 | tf_op jit(solution)/shard_map/dot_general | solution.py:80
  2302.5 30.1 %dot_general.27 = bf16[64,180,1024]{2,1,0:T(8,128)(2,1)} reshape(bf16[11520,1024]{1,0:T(8,128)(2,1)} %copy.39) | data formatting | bytes 47185920 | tf_op jit(solution)/shard_map/dot_general | solution.py:80
  2332.6 46.5 %fusion.11 = f32[64,180,1440]{2,1,0:T(8,128)} fusion(bf16[64,180,1024]{2,1,0:T(8,128)(2,1)} %dot_general.27, bf16[1024,1440]{1,0:T(8,128)(2,1)S(1)} %copy-done.2), kind=kOutput, calls=%fused_computation.21 | convolution fusion | flops 33973862400 | bytes 92897280 | tf_op jit(solution)/shard_map/dot_general | solution.py:80
  2379.2 47.9 %fusion.8 = bf16[64,180,1440]{2,0,1:T(8,128)(2,1)} fusion(f32[64,180,1440]{2,1,0:T(8,128)} %fusion.11, bf16[64,180,1440]{2,0,1:T(8,128)(2,1)} %param.5), kind=kLoop, calls=%fused_computation.11 | loop fusion | flops 182476800 | bytes 132710400 | tf_op jit(solution)/shard_map/convert_element_type | solution.py:87
  (98 shorter events, 47.2 us)
Async XLA Ops:
  0.0 1212.8 %copy-start = (bf16[256,256]{1,0:T(8,128)(2,1)S(1)}, bf16[256,256]{1,0:T(8,128)(2,1)}, u32[]{:S(2)}) copy-start(bf16[256,256]{1,0:T(8,128)(2,1)} %param.9) | copy-start | bytes 393220
  53.0 41.1 %copy-start.3 = (bf16[1024,1440]{1,0:T(8,128)(2,1)S(1)}, bf16[1024,1440]{1,0:T(8,128)(2,1)}, u32[]{:S(2)}) copy-start(bf16[1024,1440]{1,0:T(8,128)(2,1)} %convert_element_type.65) | copy-start | bytes 8847364
  242.3 9.3 copy-start.4
  242.3 773.6 %all-to-all-start = ((bf16[1,512,2,64,180]{4,3,2,0,1:T(8,128)(2,1)}), bf16[1,512,2,64,180]{4,3,2,0,1:T(8,128)(2,1)}, u32[]{:S(2)}, u32[]{:S(2)}) async-start(bf16[1,512,2,64,180]{4,3,2,0,1:T(8,128)(2,1)} %bitcast.33), calls=%async_computation | async-start | bytes 67108864 | tf_op jit(solution)/shard_map/all_to_all | solution.py:39
  1447.2 772.7 %all-to-all-start.1 = ((bf16[16,32,2,64,180]{4,3,2,1,0:T(8,128)(2,1)}), bf16[16,32,2,64,180]{4,3,2,1,0:T(8,128)(2,1)}, u32[]{:S(2)}, u32[]{:S(2)}) async-start(bf16[16,32,2,64,180]{4,3,2,1,0:T(8,128)(2,1)} %bitcast.36), calls=%async_computation.1 | async-start | bytes 67108864 | tf_op jit(solution)/shard_map/all_to_all | solution.py:78
  2302.5 30.1 %copy-start.2 = (bf16[1024,1440]{1,0:T(8,128)(2,1)S(1)}, bf16[1024,1440]{1,0:T(8,128)(2,1)}, u32[]{:S(2)}) copy-start(bf16[1024,1440]{1,0:T(8,128)(2,1)} %convert_element_type.70) | copy-start | bytes 8847364
  2379.2 47.9 %copy-start.1 = (bf16[256,256]{1,0:T(8,128)(2,1)S(1)}, bf16[256,256]{1,0:T(8,128)(2,1)}, u32[]{:S(2)}) copy-start(bf16[256,256]{1,0:T(8,128)(2,1)} %param.9) | copy-start | bytes 393220
where the time goes:
time: 2450 us; the launch traced here: 2430 us
  waiting for transfers between devices  1360 us (56%)
  local copies, waits for them, and re-layouts  780 us (32%)
  matrix products  211 us (9%)
  other arithmetic  66.4 us (3%)
    all_to_all x1, waiting for transfers between devices, shards(): lax.all_to_all(outgoing, ('lat', 'ord'), split_axis=0, concat_axis=0, til...  756 us
    all_to_all x1, waiting for transfers between devices, shards(): lax.all_to_all(fourier.reshape(1, all_slots, 2, channels, lat_rows), ('la...  600 us
    reshape x1, local copies, waits for them, and re-layouts, shards(): fourier.reshape(1, all_slots, 2, channels, lat_rows)  105 us
    mul x2, local copies, waits for them, and re-layouts, shards(): spec.reshape(my_slots, degrees, 2, width) * gain_rows[:, :, None, :]  80.1 us
    reshape x1, local copies, waits for them, and re-layouts, shards(): synth.reshape(my_slots, 2, ord_count, channels, lat_count, lat_rows)  67 us
    gather x96, local copies, waits for them, and re-layouts  66.8 us
    dot_general x2, local copies, waits for them, and re-layouts, shards(): lax.dot_general(returned, inverse.reshape(2 * all_slots, lon_count), (((0...  60.6 us
    reshape x1, local copies, waits for them, and re-layouts, shards(): gathered = arrived.reshape(my_slots, 2 * width, latitudes)  57 us
  transfers between devices with their start and end apart: 2, of which 2 were waited for; matrix products, arithmetic and copies ran while one was open for 7% of the time, Pallas kernels for 0%

commit v1 on v0

v1 whole, which is shorter than its diff:
```python
import functools
import math

import jax
import jax.numpy as jnp
from jax import lax
from jax.experimental import pallas as pl
from jax.experimental.pallas import tpu as pltpu
from jax.sharding import PartitionSpec as P

LANES = 128
VMEM = 60 * 1024 * 1024


def lane_spans(lon_count):
    return [(at, min(LANES, lon_count - at)) for at in range(0, lon_count, LANES)]


def row_tables(orders, lon_count):
    blocks = -(-lon_count // LANES)
    fine = jnp.arange(LANES, dtype=jnp.int32)
    coarse = jnp.arange(blocks, dtype=jnp.int32) * LANES
    step = jnp.concatenate([fine, coarse])
    phase = orders[:, None] * step[None, :] % lon_count
    angle = phase.astype(jnp.float32) * (2.0 * math.pi / lon_count)
    return jnp.cos(angle), jnp.sin(angle)


def table_kernel(cos_ref, sin_ref, imag_ref, weight_ref, forward_ref, inverse_ref, *, lon_count):
    fine_cos = cos_ref[:, :LANES]
    fine_sin = sin_ref[:, :LANES]
    root = 1.0 / math.sqrt(lon_count)
    imag = imag_ref[...] > 0
    weight = weight_ref[...]
    for block in range(-(-lon_count // LANES)):
        start = block * LANES
        width = min(LANES, lon_count - start)
        at = LANES + block
        c = cos_ref[:, at : at + 1]
        s = sin_ref[:, at : at + 1]
        left = jnp.where(imag, -s, c)
        right = jnp.where(imag, c, s)
        value = (left * fine_cos - right * fine_sin) * root
        forward_ref[:, start : start + width] = value[:, :width].astype(jnp.bfloat16)
        inverse_ref[:, start : start + width] = (value * weight)[:, :width].astype(jnp.bfloat16)


def build_tables(orders, imag, lon_count):
    cosine, sine = row_tables(orders, lon_count)
    rows = orders.shape[0]
    weight = jnp.where(orders == 0, 1.0, 2.0).astype(jnp.float32)[:, None]
    tile = 256 if rows % 256 == 0 else rows
    out = jax.ShapeDtypeStruct((rows, lon_count), jnp.bfloat16)
    wide = cosine.shape[1]
    return pl.pallas_call(
        functools.partial(table_kernel, lon_count=lon_count),
        grid=(rows // tile,),
        in_specs=[
            pl.BlockSpec((tile, wide), lambda i: (i, 0)),
            pl.BlockSpec((tile, wide), lambda i: (i, 0)),
            pl.BlockSpec((tile, 1), lambda i: (i, 0)),
            pl.BlockSpec((tile, 1), lambda i: (i, 0)),
        ],
        out_specs=[pl.BlockSpec((tile, lon_count), lambda i: (i, 0))] * 2,
        out_shape=[out, out],
        name="tables",
    )(cosine, sine, imag[:, None], weight)


def analysis_kernel(state_ref, table_ref, out_ref, *, group):
    rows, channels, lon_count = state_ref.shape
    targets, _, slots, _ = out_ref.shape
    half = targets * slots
    for first in range(0, rows, group):
        got = lax.dot_general(
            table_ref[...],
            state_ref[first : first + group].reshape(group * channels, lon_count),
            (((1,), (1,)), ((), ())),
            preferred_element_type=jnp.float32,
        )
        for q in range(group):
            cols = got[:, q * channels : (q + 1) * channels]
            both = jnp.concatenate([cols[:half], cols[half:]], axis=1)
            out_ref[:, first + q] = both.reshape(targets, slots, 2 * channels).astype(jnp.bfloat16)


def analyse(state, table, targets, slots, tile):
    lat_rows, channels, lon_count = state.shape
    group = math.gcd(tile, max(1, 256 // channels))
    rows = 2 * targets * slots
    return pl.pallas_call(
        functools.partial(analysis_kernel, group=group),
        grid=(lat_rows // tile,),
        in_specs=[
            pl.BlockSpec((tile, channels, lon_count), lambda i: (i, 0, 0)),
            pl.BlockSpec((rows, lon_count), lambda i: (0, 0)),
        ],
        out_specs=pl.BlockSpec((targets, tile, slots, 2 * channels), lambda i: (0, i, 0, 0)),
        out_shape=jax.ShapeDtypeStruct((targets, lat_rows, slots, 2 * channels), jnp.bfloat16),
        compiler_params=pltpu.CompilerParams(vmem_limit_bytes=VMEM),
        cost_estimate=pl.CostEstimate(
            flops=2 * rows * channels * lat_rows * lon_count,
            bytes_accessed=2 * channels * lat_rows * (lon_count + rows),
            transcendentals=0,
        ),
        name="analysis",
    )(state, table)


def legendre_kernel(order_ref, in_ref, leg_ref, gain_ref, mix_ref, out_ref, wide, xb, acc, *, part):
    _, ords, lats, rows, width = in_ref.shape
    degrees = leg_ref.shape[1]
    for o in range(ords):
        for a in range(lats):
            wide[a * rows : (a + 1) * rows, o * width : (o + 1) * width] = in_ref[0, o, a].astype(
                jnp.float32
            )
    xb[...] = wide[...].astype(jnp.bfloat16)
    order = order_ref[pl.program_id(0)]
    acc[...] = jnp.zeros_like(acc)
    for start in range(0, degrees, part):

        @pl.when(start < degrees - order)
        def _():
            leg = leg_ref[0, start : start + part, :]
            spec = jnp.dot(leg, xb[...], preferred_element_type=jnp.float32)
            at = order + start
            aligned = gain_ref[pl.ds(pl.multiple_of(at // 8 * 8, 8), part + 8), :]
            gain = pltpu.roll(aligned, part + 8 - at % 8, 0)[:part]
            row = lax.broadcasted_iota(jnp.int32, spec.shape, 0) + start
            kept = jnp.where(row < degrees - order, spec * gain, 0.0).astype(jnp.bfloat16)
            mixed = jnp.dot(kept, mix_ref[...], preferred_element_type=jnp.float32)
            acc[...] += lax.dot_general(
                leg,
                mixed.astype(jnp.bfloat16),
                (((0,), (0,)), ((), ())),
                preferred_element_type=jnp.float32,
            )

    for o in range(ords):
        for a in range(lats):
            out_ref[0, o, a] = acc[
                a * rows : (a + 1) * rows, o * width : (o + 1) * width
            ].astype(jnp.bfloat16)


def legendre_stage(coeffs, legendre, orders, gain, mix, first):
    slots, ords, lats, rows, width = coeffs.shape
    degrees, latitudes = legendre.shape[1:]
    total = ords * width
    part = degrees // 3 if degrees % 48 == 0 else degrees
    block = pl.BlockSpec((1, ords, lats, rows, width), lambda s, _: (s, 0, 0, 0, 0))
    return pl.pallas_call(
        functools.partial(legendre_kernel, part=part),
        grid_spec=pltpu.PrefetchScalarGridSpec(
            num_scalar_prefetch=1,
            grid=(slots,),
            in_specs=[
                block,
                pl.BlockSpec((1, degrees, latitudes), lambda s, _: (s + first, 0, 0)),
                pl.BlockSpec(gain.shape, lambda s, _: (0, 0)),
                pl.BlockSpec(mix.shape, lambda s, _: (0, 0)),
            ],
            out_specs=block,
            scratch_shapes=[
                pltpu.VMEM((latitudes, total), jnp.float32),
                pltpu.VMEM((latitudes, total), jnp.bfloat16),
                pltpu.VMEM((latitudes, total), jnp.float32),
            ],
        ),
        out_shape=jax.ShapeDtypeStruct(coeffs.shape, jnp.bfloat16),
        compiler_params=pltpu.CompilerParams(vmem_limit_bytes=VMEM),
        cost_estimate=pl.CostEstimate(
            flops=2 * slots * degrees * total * (2 * latitudes + total),
            bytes_accessed=2 * slots * (degrees * latitudes + 2 * latitudes * total),
            transcendentals=0,
        ),
        name="legendre",
    )(orders, coeffs, legendre, gain, mix)


def synthesis_kernel(*refs, count, group):
    chunks = refs[:count]
    table_ref, state_ref, out_ref, left = refs[count:]
    rows, channels, lon_count = state_ref.shape
    for first in range(0, rows, group):
        base = 0
        for ref in chunks:
            targets, _, slots, _ = ref.shape
            half = targets * slots
            for q in range(group):
                both = ref[:, first + q].reshape(half, 2 * channels)
                cols = slice((first + q) * channels, (first + q + 1) * channels)
                left[base : base + half, cols] = both[:, :channels]
                left[base + half : base + 2 * half, cols] = both[:, channels:]
            base += 2 * half
        x = lax.dot_general(
            left[:, first * channels : (first + group) * channels],
            table_ref[...],
            (((0,), (0,)), ((), ())),
            preferred_element_type=jnp.float32,
        )
        inner = x * (math.sqrt(2.0 / math.pi) * (1.0 + 0.044715 * (x * x)))
        y = 0.5 * x * (1.0 + jnp.tanh(inner))
        own = state_ref[first : first + group].astype(jnp.float32)
        out_ref[first : first + group] = (
            own + y.reshape(group, channels, lon_count)
        ).astype(jnp.bfloat16)


def synthesise(chunks, table, state, tile):
    lat_rows, channels, lon_count = state.shape
    group = math.gcd(tile, max(1, 256 // channels))
    block = pl.BlockSpec((tile, channels, lon_count), lambda i: (i, 0, 0))
    return pl.pallas_call(
        functools.partial(synthesis_kernel, count=len(chunks), group=group),
        grid=(lat_rows // tile,),
        in_specs=[
            pl.BlockSpec((c.shape[0], tile) + c.shape[2:], lambda i: (0, i, 0, 0)) for c in chunks
        ]
        + [pl.BlockSpec(table.shape, lambda i: (0, 0)), block],
        out_specs=block,
        out_shape=jax.ShapeDtypeStruct(state.shape, jnp.bfloat16),
        scratch_shapes=[pltpu.VMEM((table.shape[0], tile * channels), jnp.bfloat16)],
        compiler_params=pltpu.CompilerParams(vmem_limit_bytes=VMEM),
        name="synthesis",
    )(*chunks, table, state)


def shards(state_field, slot_order, legendre, degree_gain, mixing):
    channels, lat_rows, lon_count = state_field.shape
    my_slots, degrees, latitudes = legendre.shape
    width = mixing.shape[0]
    lat_count = lax.axis_size("lat")
    ord_count = lax.axis_size("ord")
    targets = lat_count * ord_count
    tile = math.gcd(lat_rows, 12)
    state = state_field.transpose(1, 0, 2)
    unit = max(8, my_slots // 4)
    sizes = [unit] * (my_slots // unit)

    by_target = slot_order.reshape(targets, my_slots)
    orders, imag = [], []
    first = 0
    for size in sizes:
        piece = by_target[:, first : first + size].reshape(-1)
        orders += [piece, piece]
        imag += [jnp.zeros_like(piece), jnp.ones_like(piece)]
        first += size
    forward, inverse = build_tables(jnp.concatenate(orders), jnp.concatenate(imag), lon_count)

    mine = lax.dynamic_index_in_dim(by_target, lax.axis_index(("lat", "ord")), 0, keepdims=False)
    gain = jnp.concatenate([degree_gain, jnp.zeros((degrees + 8, width), jnp.float32)], axis=0)
    gain = jnp.broadcast_to(
        gain.reshape(-1, ord_count, 1, channels), (gain.shape[0], ord_count, 2, channels)
    ).reshape(-1, 2 * width)
    mix = (
        mixing.reshape(ord_count, 1, channels, ord_count, 1, channels)
        * jnp.eye(2, dtype=mixing.dtype).reshape(1, 2, 1, 1, 2, 1)
    ).reshape(2 * width, 2 * width)

    returned = []
    first = 0
    row = 0
    for size in sizes:
        rows = 2 * targets * size
        sent = analyse(state, forward[row : row + rows], targets, size, tile)
        got = lax.all_to_all(sent, ("lat", "ord"), split_axis=0, concat_axis=0, tiled=True)
        got = got.reshape(lat_count, ord_count, lat_rows, size, 2 * channels)
        got = got.transpose(3, 1, 0, 2, 4)
        done = legendre_stage(got, legendre, mine[first : first + size], gain, mix, first)
        back = done.transpose(2, 1, 3, 0, 4).reshape(targets, lat_rows, size, 2 * channels)
        returned.append(
            lax.all_to_all(back, ("lat", "ord"), split_axis=0, concat_axis=0, tiled=True)
        )
        first += size
        row += rows
    return synthesise(returned, inverse, state, tile).transpose(1, 0, 2)


def solution(mesh):
    placed = (P(("batch", "ord"), "lat", None), P(), P(("lat", "ord"), None, None), P(), P())
    return jax.shard_map(
        shards,
        mesh=mesh,
        in_specs=placed,
        out_specs=P(("batch", "ord"), "lat", None),
        check_vma=False,
    )
```

time: 2450 us -> 1280 us (0.52)
  local copies, waits for them, and re-layouts: 780 us -> 72.6 us
  waiting for transfers between devices: 1360 us -> 742 us
  Pallas kernels: 0 us -> 281 us
  matrix products: 211 us -> 0 us
  blocking collectives: 0 us -> 136 us
  other arithmetic: 66.4 us -> 7.87 us
    all_to_all x2 -> x7, waiting for transfers between devices: 1360 us -> 742 us  [the longest x4 448 us: shards(): lax.all_to_all(sent, ('lat', 'ord'), split_axis=0, concat_axis=0, tiled=T...]
    reshape x8 -> x10, local copies, waits for them, and re-layouts: 456 us -> 28.8 us  [the longest x4 25.4 us: shards(): got = got.reshape(lat_count, ord_count, lat_rows, size, 2 * channels)]
    pallas_call x0 -> x10, Pallas kernels: none -> 281 us  [the longest x4 112 us: legendre_stage(): pl.pallas_call(functools.partial(legendre_kernel, part=part), grid_spec=p...]
    dot_general x5 -> x0, matrix products: 211 us -> none  [the longest x1 46.5 us: shards(): lax.dot_general(returned, inverse.reshape(2 * all_slots, lon_count), (((0...]
    all_to_all x0 -> x1, blocking collectives: none -> 136 us  [shards(): lax.all_to_all(back, ('lat', 'ord'), split_axis=0, concat_axis=0, tiled=T...]
    mul x2, local copies, waits for them, and re-layouts: 80.1 us -> 1.59 us  [shards(): mixing.reshape(ord_count, 1, channels, ord_count, 1, channels)]
    gather x96 -> x0, local copies, waits for them, and re-layouts: 66.8 us -> none
    dot_general x2 -> x0, local copies, waits for them, and re-layouts: 60.6 us -> none  [shards(): lax.dot_general(returned, inverse.reshape(2 * all_slots, lon_count), (((0...]
  transfers between devices with their start and end apart: 2 -> 7, of which waited for: 2 -> 7; matrix products, arithmetic and copies ran while one was open for 7% -> 5% of each run, Pallas kernels for 0% -> 14%
where the time goes in v1:
time: 1280 us
  waiting for transfers between devices  742 us (58%)
  Pallas kernels  281 us (22%)
  blocking collectives  136 us (11%)
  local copies, waits for them, and re-layouts  72.6 us (6%)
  starting transfers between devices  37.3 us (3%)
    all_to_all x4, waiting for transfers between devices, shards(): lax.all_to_all(sent, ('lat', 'ord'), split_axis=0, concat_axis=0, tiled=T...  448 us
    all_to_all x3, waiting for transfers between devices, shards(): lax.all_to_all(back, ('lat', 'ord'), split_axis=0, concat_axis=0, tiled=T...  294 us
    all_to_all x1, blocking collectives, shards(): lax.all_to_all(back, ('lat', 'ord'), split_axis=0, concat_axis=0, tiled=T...  136 us
    pallas_call x4, Pallas kernels, legendre_stage(): pl.pallas_call(functools.partial(legendre_kernel, part=part), grid_spec=p...  112 us
    pallas_call x4, Pallas kernels, analyse(): pl.pallas_call(functools.partial(analysis_kernel, group=group), grid=(lat...  92.2 us
    pallas_call x1, Pallas kernels, synthesise(): pl.pallas_call(functools.partial(synthesis_kernel, count=len(chunks), gro...  66.2 us
    transpose x4, local copies, waits for them, and re-layouts, shards(): done.transpose(2, 1, 3, 0, 4).reshape(targets, lat_rows, size, 2 * channels)  36.2 us
  transfers between devices with their start and end apart: 7, of which 7 were waited for; matrix products, arithmetic and copies ran while one was open for 5% of the time, Pallas kernels for 14%

profile of v1, /device:TPU:0, one launch (start us, length us, event | category | flops | bytes accessed | tf_op | source)
XLA Modules:
  0.0 1276.9 jit_solution(9961083986493887522)
XLA Ops:
  0.0 0.8 reshape.183
  0.8 0.1 concatenate.31
  0.9 0.1 reshape.187
  1.8 0.3 copy.54
  2.1 0.9 broadcast_select_fusion.weight_ref
  3.0 6.0 fusion.4
  9.0 10.5 tables.1
  19.5 3.6 fusion.7
  23.1 23.0 %analysis.7 = bf16[16,180,8,128]{3,2,1,0:T(8,128)(2,1)} custom-call(bf16[180,64,1440]{2,1,0:T(8,128)(2,1)} %bitcast.36, bf16[256,1440]{1,0:T(8,128)(2,1)} %get-tuple-element.9.table_ref), custom_call_target="tpu_custom_call" | custom-call | flops 8493465600 | bytes 39075840 | tf_op jit(solution)/shard_map/analysis/pallas_call | solution.py:91
  46.1 8.4 all-to-all-start.6
  54.5 23.1 %analysis.6 = bf16[16,180,8,128]{3,2,1,0:T(8,128)(2,1)} custom-call(bf16[180,64,1440]{2,1,0:T(8,128)(2,1)} %bitcast.37, bf16[256,1440]{1,0:T(8,128)(2,1)} %get-tuple-element.10.table_ref), custom_call_target="tpu_custom_call" | custom-call | flops 8493465600 | bytes 39075840 | tf_op jit(solution)/shard_map/analysis/pallas_call | solution.py:91
  77.6 116.6 %all-to-all-done.6 = bf16[16,180,8,128]{3,2,1,0:T(8,128)(2,1)} async-done(((bf16[16,180,8,128]{3,2,1,0:T(8,128)(2,1)}), bf16[16,180,8,128]{3,2,1,0:T(8,128)(2,1)}, u32[]{:S(2)}, u32[]{:S(2)}) %all-to-all-start.6) | async-done | bytes 5898272 | tf_op jit(solution)/shard_map/all_to_all | solution.py:268
  194.2 4.6 all-to-all-start.4
  198.8 23.0 %analysis.5 = bf16[16,180,8,128]{3,2,1,0:T(8,128)(2,1)} custom-call(bf16[180,64,1440]{2,1,0:T(8,128)(2,1)} %bitcast.38, bf16[256,1440]{1,0:T(8,128)(2,1)} %get-tuple-element.11.table_ref), custom_call_target="tpu_custom_call" | custom-call | flops 8493465600 | bytes 39075840 | tf_op jit(solution)/shard_map/analysis/pallas_call | solution.py:91
  221.9 119.0 %all-to-all-done.4 = bf16[16,180,8,128]{3,2,1,0:T(8,128)(2,1)} async-done(((bf16[16,180,8,128]{3,2,1,0:T(8,128)(2,1)}), bf16[16,180,8,128]{3,2,1,0:T(8,128)(2,1)}, u32[]{:S(2)}, u32[]{:S(2)}) %all-to-all-start.4) | async-done | bytes 5898272 | tf_op jit(solution)/shard_map/all_to_all | solution.py:268
  340.9 4.6 all-to-all-start.2
  345.6 23.0 %analysis.4 = bf16[16,180,8,128]{3,2,1,0:T(8,128)(2,1)} custom-call(bf16[180,64,1440]{2,1,0:T(8,128)(2,1)} %bitcast.39, bf16[256,1440]{1,0:T(8,128)(2,1)} %get-tuple-element.12.table_ref), custom_call_target="tpu_custom_call" | custom-call | flops 8493465600 | bytes 39075840 | tf_op jit(solution)/shard_map/analysis/pallas_call | solution.py:91
  368.6 119.1 %all-to-all-done.2 = bf16[16,180,8,128]{3,2,1,0:T(8,128)(2,1)} async-done(((bf16[16,180,8,128]{3,2,1,0:T(8,128)(2,1)}), bf16[16,180,8,128]{3,2,1,0:T(8,128)(2,1)}, u32[]{:S(2)}, u32[]{:S(2)}) %all-to-all-start.2) | async-done | bytes 5898272 | tf_op jit(solution)/shard_map/all_to_all | solution.py:268
  487.7 5.1 all-to-all-start
  492.9 0.2 mul.51
  493.0 0.9 broadcast_multiply_fusion
  494.0 1.4 mul.55.mix_ref
  495.4 0.3 copy.56
  495.7 0.2 concatenate.33
  495.9 0.5 broadcast_in_dim.22
  496.4 2.4 copy.57.gain_ref
  498.8 0.7 slice_bitcast_fusion
  499.4 6.3 copy.72
  505.8 27.0 %legendre.7 = bf16[8,4,4,180,128]{4,3,2,1,0:T(8,128)(2,1)} custom-call(s32[8]{0:T(128)} %get-tuple-element.19.order_ref, bf16[8,4,4,180,128]{4,3,2,1,0:T(8,128)(2,1)} %bitcast.43, bf16[32,720,720]{2,1,0:T(8,128)(2,1)} %leg_ref.7, f32[1448,512]{1,0:T(8,128)} %copy.57.gain_ref, bf16[512,512]{1,0:T(8,128)(2,1)} %mul.55.mix_ref), custom_call_target="tpu_custom_call" | custom-call | flops 11513364480 | bytes 20090880 | tf_op jit(solution)/shard_map/legendre/pallas_call | solution.py:153
  532.8 9.1 copy.67
  541.9 92.8 %all-to-all-done = bf16[16,180,8,128]{3,2,1,0:T(8,128)(2,1)} async-done(((bf16[16,180,8,128]{3,2,1,0:T(8,128)(2,1)}), bf16[16,180,8,128]{3,2,1,0:T(8,128)(2,1)}, u32[]{:S(2)}, u32[]{:S(2)}) %all-to-all-start) | async-done | bytes 5898272 | tf_op jit(solution)/shard_map/all_to_all | solution.py:268
  634.7 4.8 all-to-all-start.7
  639.5 6.3 copy.73
  645.9 26.8 %legendre.6 = bf16[8,4,4,180,128]{4,3,2,1,0:T(8,128)(2,1)} custom-call(s32[8]{0:T(128)} %get-tuple-element.20.order_ref, bf16[8,4,4,180,128]{4,3,2,1,0:T(8,128)(2,1)} %bitcast.45, bf16[32,720,720]{2,1,0:T(8,128)(2,1)} %leg_ref.7, f32[1448,512]{1,0:T(8,128)} %copy.57.gain_ref, bf16[512,512]{1,0:T(8,128)(2,1)} %mul.55.mix_ref), custom_call_target="tpu_custom_call" | custom-call | flops 11513364480 | bytes 20090880 | tf_op jit(solution)/shard_map/legendre/pallas_call | solution.py:153
  672.7 9.0 copy.64
  681.7 99.7 %all-to-all-done.7.refs_3_ = bf16[16,180,8,128]{3,2,1,0:T(8,128)(2,1)} async-done(((bf16[16,180,8,128]{3,2,1,0:T(8,128)(2,1)}), bf16[16,180,8,128]{3,2,1,0:T(8,128)(2,1)}, u32[]{:S(2)}, u32[]{:S(2)}) %all-to-all-start.7) | async-done | bytes 5898272 | tf_op jit(solution)/shard_map/all_to_all | solution.py:274
  781.4 4.8 all-to-all-start.5
  786.2 6.3 copy.74
  792.6 28.7 %legendre.5 = bf16[8,4,4,180,128]{4,3,2,1,0:T(8,128)(2,1)} custom-call(s32[8]{0:T(128)} %get-tuple-element.21.order_ref, bf16[8,4,4,180,128]{4,3,2,1,0:T(8,128)(2,1)} %bitcast.47, bf16[32,720,720]{2,1,0:T(8,128)(2,1)} %leg_ref.7, f32[1448,512]{1,0:T(8,128)} %copy.57.gain_ref, bf16[512,512]{1,0:T(8,128)(2,1)} %mul.55.mix_ref), custom_call_target="tpu_custom_call" | custom-call | flops 11513364480 | bytes 20090880 | tf_op jit(solution)/shard_map/legendre/pallas_call | solution.py:153
  821.3 9.0 copy.61
  830.3 97.8 %all-to-all-done.5.refs_2_ = bf16[16,180,8,128]{3,2,1,0:T(8,128)(2,1)} async-done(((bf16[16,180,8,128]{3,2,1,0:T(8,128)(2,1)}), bf16[16,180,8,128]{3,2,1,0:T(8,128)(2,1)}, u32[]{:S(2)}, u32[]{:S(2)}) %all-to-all-start.5) | async-done | bytes 5898272 | tf_op jit(solution)/shard_map/all_to_all | solution.py:274
  928.1 4.9 all-to-all-start.3
  933.0 6.3 copy.75
  939.3 29.7 %legendre.4 = bf16[8,4,4,180,128]{4,3,2,1,0:T(8,128)(2,1)} custom-call(s32[8]{0:T(128)} %get-tuple-element.22.order_ref, bf16[8,4,4,180,128]{4,3,2,1,0:T(8,128)(2,1)} %bitcast.41, bf16[32,720,720]{2,1,0:T(8,128)(2,1)} %leg_ref.7, f32[1448,512]{1,0:T(8,128)} %copy.57.gain_ref, bf16[512,512]{1,0:T(8,128)(2,1)} %mul.55.mix_ref), custom_call_target="tpu_custom_call" | custom-call | flops 11513364480 | bytes 20090880 | tf_op jit(solution)/shard_map/legendre/pallas_call | solution.py:153
  969.0 9.1 copy.58
  978.1 96.8 %all-to-all-done.3.refs_1_ = bf16[16,180,8,128]{3,2,1,0:T(8,128)(2,1)} async-done(((bf16[16,180,8,128]{3,2,1,0:T(8,128)(2,1)}), bf16[16,180,8,128]{3,2,1,0:T(8,128)(2,1)}, u32[]{:S(2)}, u32[]{:S(2)}) %all-to-all-start.3) | async-done | bytes 5898272 | tf_op jit(solution)/shard_map/all_to_all | solution.py:274
  1074.9 135.5 %all_to_all.40.refs_0_ = bf16[16,180,8,128]{3,2,1,0:T(8,128)(2,1)} all-to-all(bf16[16,180,8,128]{3,2,1,0:T(8,128)(2,1)} %bitcast.52), channel_id=1, replica_groups=mesh['lat'=4,'ord'=4,'batch'=2] {'lat','ord'}, dimensions={0} | all-to-all | bytes 11796480 | tf_op jit(solution)/shard_map/all_to_all | solution.py:274
  1210.4 66.2 %synthesis.1 = bf16[180,64,1440]{2,1,0:T(8,128)(2,1)} custom-call(bf16[16,180,8,128]{3,2,1,0:T(8,128)(2,1)} %all_to_all.40.refs_0_, bf16[16,180,8,128]{3,2,1,0:T(8,128)(2,1)} %all-to-all-done.3.refs_1_, bf16[16,180,8,128]{3,2,1,0:T(8,128)(2,1)} %all-to-all-done.5.refs_2_, bf16[16,180,8,128]{3,2,1,0:T(8,128)(2,1)} %all-to-all-done.7.refs_3_, ...), custom_call_target="tpu_custom_call" | custom-call | tf_op jit(solution)/shard_map/synthesis/pallas_call | solution.py:215
  (34 shorter events, 0.8 us)
Async XLA Ops:
  46.1 148.1 %all-to-all-start.6 = ((bf16[16,180,8,128]{3,2,1,0:T(8,128)(2,1)}), bf16[16,180,8,128]{3,2,1,0:T(8,128)(2,1)}, u32[]{:S(2)}, u32[]{:S(2)}) async-start(bf16[16,180,8,128]{3,2,1,0:T(8,128)(2,1)} %analysis.7), calls=%async_computation.6 | async-start | bytes 11796480 | tf_op jit(solution)/shard_map/all_to_all | solution.py:268
  194.2 146.7 %all-to-all-start.4 = ((bf16[16,180,8,128]{3,2,1,0:T(8,128)(2,1)}), bf16[16,180,8,128]{3,2,1,0:T(8,128)(2,1)}, u32[]{:S(2)}, u32[]{:S(2)}) async-start(bf16[16,180,8,128]{3,2,1,0:T(8,128)(2,1)} %analysis.6), calls=%async_computation.4 | async-start | bytes 11796480 | tf_op jit(solution)/shard_map/all_to_all | solution.py:268
  340.9 146.8 %all-to-all-start.2 = ((bf16[16,180,8,128]{3,2,1,0:T(8,128)(2,1)}), bf16[16,180,8,128]{3,2,1,0:T(8,128)(2,1)}, u32[]{:S(2)}, u32[]{:S(2)}) async-start(bf16[16,180,8,128]{3,2,1,0:T(8,128)(2,1)} %analysis.5), calls=%async_computation.2 | async-start | bytes 11796480 | tf_op jit(solution)/shard_map/all_to_all | solution.py:268
  368.6 124.2 %copy-start.1 = (bf16[256,256]{1,0:T(8,128)(2,1)S(1)}, bf16[256,256]{1,0:T(8,128)(2,1)}, u32[]{:S(2)}) copy-start(bf16[256,256]{1,0:T(8,128)(2,1)} %param.9) | copy-start | bytes 393220
  368.6 126.8 %copy-start = (f32[720,256]{1,0:T(8,128)S(1)}, f32[720,256]{1,0:T(8,128)}, u32[]{:S(2)}) copy-start(f32[720,256]{1,0:T(8,128)} %param.8) | copy-start | bytes 2211844
  487.7 147.0 %all-to-all-start = ((bf16[16,180,8,128]{3,2,1,0:T(8,128)(2,1)}), bf16[16,180,8,128]{3,2,1,0:T(8,128)(2,1)}, u32[]{:S(2)}, u32[]{:S(2)}) async-start(bf16[16,180,8,128]{3,2,1,0:T(8,128)(2,1)} %analysis.4), calls=%async_computation | async-start | bytes 11796480 | tf_op jit(solution)/shard_map/all_to_all | solution.py:268
  634.7 146.7 %all-to-all-start.7 = ((bf16[16,180,8,128]{3,2,1,0:T(8,128)(2,1)}), bf16[16,180,8,128]{3,2,1,0:T(8,128)(2,1)}, u32[]{:S(2)}, u32[]{:S(2)}) async-start(bf16[16,180,8,128]{3,2,1,0:T(8,128)(2,1)} %bitcast.50), calls=%async_computation.7 | async-start | bytes 11796480 | tf_op jit(solution)/shard_map/all_to_all | solution.py:274
  781.4 146.7 %all-to-all-start.5 = ((bf16[16,180,8,128]{3,2,1,0:T(8,128)(2,1)}), bf16[16,180,8,128]{3,2,1,0:T(8,128)(2,1)}, u32[]{:S(2)}, u32[]{:S(2)}) async-start(bf16[16,180,8,128]{3,2,1,0:T(8,128)(2,1)} %bitcast.51), calls=%async_computation.5 | async-start | bytes 11796480 | tf_op jit(solution)/shard_map/all_to_all | solution.py:274
  928.1 146.8 %all-to-all-start.3 = ((bf16[16,180,8,128]{3,2,1,0:T(8,128)(2,1)}), bf16[16,180,8,128]{3,2,1,0:T(8,128)(2,1)}, u32[]{:S(2)}, u32[]{:S(2)}) async-start(bf16[16,180,8,128]{3,2,1,0:T(8,128)(2,1)} %bitcast.49), calls=%async_computation.3 | async-start | bytes 11796480 | tf_op jit(solution)/shard_map/all_to_all | solution.py:274

commit v2 on v1

--- a/solution.py
+++ b/solution.py
@@ -9,6 +9,7 @@
 from jax.sharding import PartitionSpec as P
 
 LANES = 128
+SHARE_LATE = 14
 VMEM = 60 * 1024 * 1024
 
 
@@ -26,45 +27,28 @@
     return jnp.cos(angle), jnp.sin(angle)
 
 
-def table_kernel(cos_ref, sin_ref, imag_ref, weight_ref, forward_ref, inverse_ref, *, lon_count):
+def table_kernel(cos_ref, sin_ref, forward_ref, *, lon_count):
+    half = cos_ref.shape[0]
     fine_cos = cos_ref[:, :LANES]
     fine_sin = sin_ref[:, :LANES]
     root = 1.0 / math.sqrt(lon_count)
-    imag = imag_ref[...] > 0
-    weight = weight_ref[...]
-    for block in range(-(-lon_count // LANES)):
-        start = block * LANES
-        width = min(LANES, lon_count - start)
+    for block, (start, width) in enumerate(lane_spans(lon_count)):
         at = LANES + block
-        c = cos_ref[:, at : at + 1]
-        s = sin_ref[:, at : at + 1]
-        left = jnp.where(imag, -s, c)
-        right = jnp.where(imag, c, s)
-        value = (left * fine_cos - right * fine_sin) * root
-        forward_ref[:, start : start + width] = value[:, :width].astype(jnp.bfloat16)
-        inverse_ref[:, start : start + width] = (value * weight)[:, :width].astype(jnp.bfloat16)
-
-
-def build_tables(orders, imag, lon_count):
+        c = cos_ref[:, at : at + 1] * root
+        s = sin_ref[:, at : at + 1] * root
+        real = c * fine_cos - s * fine_sin
+        imag = -(s * fine_cos + c * fine_sin)
+        forward_ref[:half, start : start + width] = real[:, :width].astype(jnp.bfloat16)
+        forward_ref[half:, start : start + width] = imag[:, :width].astype(jnp.bfloat16)
+
+
+def build_table(orders, lon_count):
     cosine, sine = row_tables(orders, lon_count)
-    rows = orders.shape[0]
-    weight = jnp.where(orders == 0, 1.0, 2.0).astype(jnp.float32)[:, None]
-    tile = 256 if rows % 256 == 0 else rows
-    out = jax.ShapeDtypeStruct((rows, lon_count), jnp.bfloat16)
-    wide = cosine.shape[1]
     return pl.pallas_call(
         functools.partial(table_kernel, lon_count=lon_count),
-        grid=(rows // tile,),
-        in_specs=[
-            pl.BlockSpec((tile, wide), lambda i: (i, 0)),
-            pl.BlockSpec((tile, wide), lambda i: (i, 0)),
-            pl.BlockSpec((tile, 1), lambda i: (i, 0)),
-            pl.BlockSpec((tile, 1), lambda i: (i, 0)),
-        ],
-        out_specs=[pl.BlockSpec((tile, lon_count), lambda i: (i, 0))] * 2,
-        out_shape=[out, out],
-        name="tables",
-    )(cosine, sine, imag[:, None], weight)
+        out_shape=jax.ShapeDtypeStruct((2 * orders.shape[0], lon_count), jnp.bfloat16),
+        name="table",
+    )(cosine, sine)
 
 
 def analysis_kernel(state_ref, table_ref, out_ref, *, group):
@@ -181,7 +165,8 @@
 
 def synthesis_kernel(*refs, count, group):
     chunks = refs[:count]
-    table_ref, state_ref, out_ref, left = refs[count:]
+    table_ref, state_ref = refs[count : count + 2]
+    out_ref, left = refs[-2:]
     rows, channels, lon_count = state_ref.shape
     for first in range(0, rows, group):
         base = 0
@@ -208,23 +193,39 @@
         ).astype(jnp.bfloat16)
 
 
-def synthesise(chunks, table, state, tile):
+def synthesise(chunks, table, state, tile, starts, first, count, filled=None):
     lat_rows, channels, lon_count = state.shape
     group = math.gcd(tile, max(1, 256 // channels))
-    block = pl.BlockSpec((tile, channels, lon_count), lambda i: (i, 0, 0))
+    block = pl.BlockSpec((tile, channels, lon_count), lambda i: (i + first, 0, 0))
+
+    def rows_of(shape, start):
+        return pl.BlockSpec((shape[0], tile) + shape[2:], lambda i: (0, i + first - start, 0, 0))
+
+    operands = [*chunks, table, state]
+    specs = [rows_of(c.shape, start) for c, start in zip(chunks, starts)]
+    specs += [pl.BlockSpec(table.shape, lambda i: (0, 0)), block]
+    aliases = {}
+    if filled is not None:
+        aliases = {len(operands): 0}
+        operands.append(filled)
+        specs.append(pl.BlockSpec(memory_space=pl.ANY))
+    lats = count * tile
     return pl.pallas_call(
         functools.partial(synthesis_kernel, count=len(chunks), group=group),
-        grid=(lat_rows // tile,),
-        in_specs=[
-            pl.BlockSpec((c.shape[0], tile) + c.shape[2:], lambda i: (0, i, 0, 0)) for c in chunks
-        ]
-        + [pl.BlockSpec(table.shape, lambda i: (0, 0)), block],
+        grid=(count,),
+        in_specs=specs,
         out_specs=block,
         out_shape=jax.ShapeDtypeStruct(state.shape, jnp.bfloat16),
         scratch_shapes=[pltpu.VMEM((table.shape[0], tile * channels), jnp.bfloat16)],
+        input_output_aliases=aliases,
         compiler_params=pltpu.CompilerParams(vmem_limit_bytes=VMEM),
+        cost_estimate=pl.CostEstimate(
+            flops=2 * table.shape[0] * channels * lats * lon_count,
+            bytes_accessed=2 * channels * lats * (2 * lon_count + table.shape[0]),
+            transcendentals=channels * lats * lon_count,
+        ),
         name="synthesis",
-    )(*chunks, table, state)
+    )(*operands)
 
 
 def shards(state_field, slot_order, legendre, degree_gain, mixing):
@@ -235,19 +236,12 @@
     ord_count = lax.axis_size("ord")
     targets = lat_count * ord_count
     tile = math.gcd(lat_rows, 12)
+    wide_tile = math.gcd(lat_rows, 20)
     state = state_field.transpose(1, 0, 2)
     unit = max(8, my_slots // 4)
-    sizes = [unit] * (my_slots // unit)
+    sizes = [size for size in (unit, my_slots - unit) if size > 0]
 
     by_target = slot_order.reshape(targets, my_slots)
-    orders, imag = [], []
-    first = 0
-    for size in sizes:
-        piece = by_target[:, first : first + size].reshape(-1)
-        orders += [piece, piece]
-        imag += [jnp.zeros_like(piece), jnp.ones_like(piece)]
-        first += size
-    forward, inverse = build_tables(jnp.concatenate(orders), jnp.concatenate(imag), lon_count)
 
     mine = lax.dynamic_index_in_dim(by_target, lax.axis_index(("lat", "ord")), 0, keepdims=False)
     gain = jnp.concatenate([degree_gain, jnp.zeros((degrees + 8, width), jnp.float32)], axis=0)
@@ -259,23 +253,53 @@
         * jnp.eye(2, dtype=mixing.dtype).reshape(1, 2, 1, 1, 2, 1)
     ).reshape(2 * width, 2 * width)
 
-    returned = []
+    steps = lat_rows // tile
+    late = max(1, SHARE_LATE * steps // 100) if steps > 1 else 0
+    early_rows = (steps - late) * tile
+    exchange = functools.partial(
+        lax.all_to_all, axis_name=("lat", "ord"), split_axis=0, concat_axis=0, tiled=True
+    )
+    tables, weights, arrived = [], [], []
     first = 0
-    row = 0
     for size in sizes:
-        rows = 2 * targets * size
-        sent = analyse(state, forward[row : row + rows], targets, size, tile)
-        got = lax.all_to_all(sent, ("lat", "ord"), split_axis=0, concat_axis=0, tiled=True)
+        orders = by_target[:, first : first + size].reshape(-1)
+        tables.append(build_table(orders, lon_count))
+        weights += [jnp.where(orders == 0, 1.0, 2.0)] * 2
+        sent = analyse(state, tables[-1], targets, size, wide_tile)
+        if arrived:
+            sent, arrived[-1] = lax.optimization_barrier((sent, arrived[-1]))
+        arrived.append(exchange(sent))
+        first += size
+
+    backs = []
+    first = 0
+    for size, got in zip(sizes, arrived):
         got = got.reshape(lat_count, ord_count, lat_rows, size, 2 * channels)
         got = got.transpose(3, 1, 0, 2, 4)
         done = legendre_stage(got, legendre, mine[first : first + size], gain, mix, first)
-        back = done.transpose(2, 1, 3, 0, 4).reshape(targets, lat_rows, size, 2 * channels)
-        returned.append(
-            lax.all_to_all(back, ("lat", "ord"), split_axis=0, concat_axis=0, tiled=True)
-        )
+        backs.append(done.transpose(2, 1, 3, 0, 4).reshape(targets, lat_rows, size, 2 * channels))
         first += size
-        row += rows
-    return synthesise(returned, inverse, state, tile).transpose(1, 0, 2)
+    inverse = (
+        jnp.concatenate(tables, axis=0) * jnp.concatenate(weights)[:, None]
+    ).astype(jnp.bfloat16)
+
+    settled = [exchange(back) for back in backs[:-1]]
+    zeros = [0] * len(settled)
+    if not late:
+        every = settled + [exchange(backs[-1])]
+        out = synthesise(every, inverse, state, tile, zeros + [0], 0, steps)
+        return out.transpose(1, 0, 2)
+    early, rest = backs[-1][:, :early_rows], backs[-1][:, early_rows:]
+    if settled:
+        early, rest, settled[-1] = lax.optimization_barrier((early, rest, settled[-1]))
+    early = exchange(early)
+    early, rest = lax.optimization_barrier((early, rest))
+    rest = exchange(rest)
+    out = synthesise(settled + [early], inverse, state, tile, zeros + [0], 0, steps - late)
+    out = synthesise(
+        settled + [rest], inverse, state, tile, zeros + [steps - late], steps - late, late, out
+    )
+    return out.transpose(1, 0, 2)
 
 
 def solution(mesh):

time: 1280 us -> 1150 us (0.90)
  waiting for transfers between devices: 742 us -> 496 us
  blocking collectives: 136 us -> 339 us
  Pallas kernels: 281 us -> 229 us
  local copies, waits for them, and re-layouts: 72.6 us -> 57.6 us
  starting transfers between devices: 37.3 us -> 23.4 us
    all_to_all x7 -> x4, waiting for transfers between devices: 742 us -> 496 us  [the longest x2 459 us: shards(): arrived.append(exchange(sent))]
    all_to_all x1, blocking collectives: 136 us -> 339 us  [shards(): early = exchange(early)]
    pallas_call x4 -> x2, Pallas kernels: 92.2 us -> 53.8 us  [analyse(): pl.pallas_call(functools.partial(analysis_kernel, group=group), grid=(lat...]
    transpose x4 -> x2, local copies, waits for them, and re-layouts: 36.2 us -> 20.4 us  [shards(): done.transpose(2, 1, 3, 0, 4).reshape(targets, lat_rows, size, 2 * channels)]
    all_to_all x7 -> x4, starting transfers between devices: 37.3 us -> 23.4 us  [the longest x2 13.8 us: shards(): arrived.append(exchange(sent))]
    pallas_call x4 -> x2, Pallas kernels: 112 us -> 98.6 us  [legendre_stage(): pl.pallas_call(functools.partial(legendre_kernel, part=part), grid_spec=p...]
    pallas_call x1 -> x2, Pallas kernels: 66.2 us -> 70.1 us  [synthesise(): pl.pallas_call(functools.partial(synthesis_kernel, count=len(chunks), gro...]
  transfers between devices with their start and end apart: 7 -> 4, of which waited for: 7 -> 3; matrix products, arithmetic and copies ran while one was open for 5% -> 5% of each run, Pallas kernels for 14% -> 17%
where the time goes in v2:
time: 1150 us
  waiting for transfers between devices  496 us (43%)
  blocking collectives  339 us (29%)
  Pallas kernels  229 us (20%)
  local copies, waits for them, and re-layouts  57.6 us (5%)
  starting transfers between devices  23.4 us (2%)
    all_to_all x2, waiting for transfers between devices, shards(): arrived.append(exchange(sent))  459 us
    all_to_all x1, blocking collectives, shards(): early = exchange(early)  339 us
    pallas_call x2, Pallas kernels, legendre_stage(): pl.pallas_call(functools.partial(legendre_kernel, part=part), grid_spec=p...  98.6 us
    pallas_call x2, Pallas kernels, synthesise(): pl.pallas_call(functools.partial(synthesis_kernel, count=len(chunks), gro...  70.1 us
    pallas_call x2, Pallas kernels, analyse(): pl.pallas_call(functools.partial(analysis_kernel, group=group), grid=(lat...  53.8 us
    all_to_all x1, waiting for transfers between devices, shards(): settled = [exchange(back) for back in backs[:-1]]  36.3 us
  transfers between devices with their start and end apart: 4, of which 3 were waited for; matrix products, arithmetic and copies ran while one was open for 5% of the time, Pallas kernels for 17%

profile of v2, /device:TPU:0, one launch (start us, length us, event | category | flops | bytes accessed | tf_op | source)
XLA Modules:
  0.0 1151.9 jit_solution(17036827068933170460)
XLA Ops:
  0.0 0.8 reshape.70
  0.8 0.1 mul.84
  0.9 0.0 copy-start.4
  0.9 1.3 fusion.11
  2.2 2.4 table.3.table_ref
  4.6 19.5 %analysis.3 = bf16[16,180,8,128]{3,2,1,0:T(8,128)(2,1)} custom-call(bf16[180,64,1440]{2,1,0:T(8,128)(2,1)} %bitcast.21, bf16[256,1440]{1,0:T(8,128)(2,1)} %table.3.table_ref), custom_call_target="tpu_custom_call" | custom-call | flops 8493465600 | bytes 39075840 | tf_op jit(solution)/shard_map/analysis/pallas_call | solution.py:75
  24.1 0.0 copy-done.4
  24.1 8.4 all-to-all-start
  32.5 0.1 slice.32
  32.6 0.1 mul.77
  32.7 2.7 fusion.4
  35.4 3.9 table.2.table_ref
  39.3 34.3 %analysis.2 = bf16[16,180,24,128]{3,2,1,0:T(8,128)(2,1)} custom-call(bf16[180,64,1440]{2,1,0:T(8,128)(2,1)} %bitcast.22, bf16[768,1440]{1,0:T(8,128)(2,1)} %table.2.table_ref), custom_call_target="tpu_custom_call" | custom-call | flops 25480396800 | bytes 50872320 | tf_op jit(solution)/shard_map/analysis/pallas_call | solution.py:75
  73.6 0.0 copy-start.3
  73.6 98.6 %all-to-all-done = bf16[16,180,8,128]{3,2,1,0:T(8,128)(2,1)} async-done(((bf16[16,180,8,128]{3,2,1,0:T(8,128)(2,1)}), bf16[16,180,8,128]{3,2,1,0:T(8,128)(2,1)}, u32[]{:S(2)}, u32[]{:S(2)}) %all-to-all-start) | async-done | bytes 5898272 | tf_op jit(solution)/shard_map/all_to_all | solution.py:271
  172.2 5.4 all-to-all-start.1
  177.6 0.0 copy-done.3
  177.6 0.2 mul.90
  177.8 0.9 broadcast_multiply_fusion
  178.7 1.4 mul.94.mix_ref
  180.2 0.0 copy-done.2
  180.2 0.3 copy.10
  180.4 0.2 concatenate.19
  180.6 0.5 broadcast_in_dim.28
  181.1 2.4 copy.11.gain_ref
  183.5 0.5 slice_bitcast_fusion.order_ref
  184.1 6.3 copy.19
  190.4 28.7 %legendre.3 = bf16[8,4,4,180,128]{4,3,2,1,0:T(8,128)(2,1)} custom-call(s32[8]{0:T(128)} %slice_bitcast_fusion.order_ref, bf16[8,4,4,180,128]{4,3,2,1,0:T(8,128)(2,1)} %bitcast.27, bf16[32,720,720]{2,1,0:T(8,128)(2,1)} %leg_ref.3, f32[1448,512]{1,0:T(8,128)} %copy.11.gain_ref, bf16[512,512]{1,0:T(8,128)(2,1)} %mul.94.mix_ref), custom_call_target="tpu_custom_call" | custom-call | flops 11513364480 | bytes 20090880 | tf_op jit(solution)/shard_map/legendre/pallas_call | solution.py:137
  219.1 9.0 copy.15
  228.1 360.7 %all-to-all-done.1 = bf16[16,180,24,128]{3,2,1,0:T(8,128)(2,1)} async-done(((bf16[16,180,24,128]{3,2,1,0:T(8,128)(2,1)}), bf16[16,180,24,128]{3,2,1,0:T(8,128)(2,1)}, u32[]{:S(2)}, u32[]{:S(2)}) %all-to-all-start.1) | async-done | bytes 17694752 | tf_op jit(solution)/shard_map/all_to_all | solution.py:271
  588.8 4.8 all-to-all-start.2
  593.6 0.7 slice_bitcast_fusion.1.order_ref
  594.3 15.9 %copy.18 = bf16[4,4,180,24,128]{4,2,0,1,3:T(8,128)(2,1)} copy(bf16[4,4,180,24,128]{4,3,2,1,0:T(8,128)(2,1)} %bitcast.2) | data formatting | bytes 35389440 | tf_op jit(solution)/shard_map/reshape | solution.py:277
  610.2 69.9 %legendre.2 = bf16[24,4,4,180,128]{4,3,2,1,0:T(8,128)(2,1)} custom-call(s32[24]{0:T(128)} %slice_bitcast_fusion.1.order_ref, bf16[24,4,4,180,128]{4,3,2,1,0:T(8,128)(2,1)} %bitcast.30, bf16[32,720,720]{2,1,0:T(8,128)(2,1)} %leg_ref.3, f32[1448,512]{1,0:T(8,128)} %copy.11.gain_ref, bf16[512,512]{1,0:T(8,128)(2,1)} %mul.94.mix_ref), custom_call_target="tpu_custom_call" | custom-call | flops 34540093440 | bytes 60272640 | tf_op jit(solution)/shard_map/legendre/pallas_call | solution.py:137
  680.1 11.4 copy.12
  691.5 2.0 slice.35
  693.5 5.8 slice.34
  699.3 0.0 copy-start.5
  699.3 36.3 %all-to-all-done.2.refs_0_ = bf16[16,180,8,128]{3,2,1,0:T(8,128)(2,1)} async-done(((bf16[16,180,8,128]{3,2,1,0:T(8,128)(2,1)}), bf16[16,180,8,128]{3,2,1,0:T(8,128)(2,1)}, u32[]{:S(2)}, u32[]{:S(2)}) %all-to-all-start.2) | async-done | bytes 5898272 | tf_op jit(solution)/shard_map/all_to_all | solution.py:286
  735.6 339.0 %all_to_all.25.refs_1_ = bf16[16,156,24,128]{3,2,1,0:T(8,128)(2,1)} all-to-all(bf16[16,156,24,128]{3,2,1,0:T(8,128)(2,1)} %slice.34), channel_id=1, replica_groups=mesh['lat'=4,'ord'=4,'batch'=2] {'lat','ord'}, dimensions={0} | all-to-all | bytes 30670848 | tf_op jit(solution)/shard_map/all_to_all | solution.py:295
  1074.6 4.9 all-to-all-start.4
  1079.4 0.0 copy-done.5
  1079.5 0.0 copy-done.1
  1079.5 0.0 copy-done
  1079.5 2.3 maximum_multiply_fusion.refs_2_
  1081.8 57.5 %synthesis.2.refs_4_ = bf16[180,64,1440]{2,1,0:T(8,128)(2,1)} custom-call(bf16[16,180,8,128]{3,2,1,0:T(8,128)(2,1)} %all-to-all-done.2.refs_0_, bf16[16,156,24,128]{3,2,1,0:T(8,128)(2,1)} %all_to_all.25.refs_1_, bf16[1024,1440]{1,0:T(8,128)(2,1)} %maximum_multiply_fusion.refs_2_, bf16[180,64,1440]{2,1,0:T(8,128)(2,1)} %bitcast.23), custom_call_target="tpu_custom_call" | custom-call | flops 29444014080 | bytes 77955072 | tf_op jit(solution)/shard_map/synthesis/pallas_call | solution.py:213
  1139.3 0.0 all-to-all-done.4.refs_1_
  1139.3 12.7 %synthesis.3 = bf16[180,64,1440]{2,1,0:T(8,128)(2,1)} custom-call(bf16[16,180,8,128]{3,2,1,0:T(8,128)(2,1)} %all-to-all-done.2.refs_0_, bf16[16,24,24,128]{3,2,1,0:T(8,128)(2,1)} %all-to-all-done.4.refs_1_, bf16[1024,1440]{1,0:T(8,128)(2,1)} %maximum_multiply_fusion.refs_2_, bf16[180,64,1440]{2,1,0:T(8,128)(2,1)} %bitcast.24, ...), custom_call_target="tpu_custom_call", output_to_operand_aliasing={{}: (4, {})} | custom-call | flops 4529848320 | bytes 11993088 | tf_op jit(solution)/shard_map/synthesis/pallas_call | solution.py:213
  (11 shorter events, 0.1 us)
Async XLA Ops:
  0.9 23.3 %copy-start.4 = (s32[128]{0:T(128)}, s32[128]{0:T(128)S(1)}, u32[]{:S(2)}) copy-start(s32[128]{0:T(128)S(1)} %mul.84) | copy-start | bytes 1540
  24.1 148.1 %all-to-all-start = ((bf16[16,180,8,128]{3,2,1,0:T(8,128)(2,1)}), bf16[16,180,8,128]{3,2,1,0:T(8,128)(2,1)}, u32[]{:S(2)}, u32[]{:S(2)}) async-start(bf16[16,180,8,128]{3,2,1,0:T(8,128)(2,1)} %analysis.3), calls=%async_computation | async-start | bytes 11796480 | tf_op jit(solution)/shard_map/all_to_all | solution.py:271
  73.6 104.0 %copy-start.3 = (bf16[256,256]{1,0:T(8,128)(2,1)S(1)}, bf16[256,256]{1,0:T(8,128)(2,1)}, u32[]{:S(2)}) copy-start(bf16[256,256]{1,0:T(8,128)(2,1)} %param.9) | copy-start | bytes 393220
  73.6 106.6 %copy-start.2 = (f32[720,256]{1,0:T(8,128)S(1)}, f32[720,256]{1,0:T(8,128)}, u32[]{:S(2)}) copy-start(f32[720,256]{1,0:T(8,128)} %param.8) | copy-start | bytes 2211844
  172.2 416.6 %all-to-all-start.1 = ((bf16[16,180,24,128]{3,2,1,0:T(8,128)(2,1)}), bf16[16,180,24,128]{3,2,1,0:T(8,128)(2,1)}, u32[]{:S(2)}, u32[]{:S(2)}) async-start(bf16[16,180,24,128]{3,2,1,0:T(8,128)(2,1)} %analysis.2), calls=%async_computation.1 | async-start | bytes 35389440 | tf_op jit(solution)/shard_map/all_to_all | solution.py:271
  588.8 146.8 %all-to-all-start.2 = ((bf16[16,180,8,128]{3,2,1,0:T(8,128)(2,1)}), bf16[16,180,8,128]{3,2,1,0:T(8,128)(2,1)}, u32[]{:S(2)}, u32[]{:S(2)}) async-start(bf16[16,180,8,128]{3,2,1,0:T(8,128)(2,1)} %bitcast.29), calls=%async_computation.2 | async-start | bytes 11796480 | tf_op jit(solution)/shard_map/all_to_all | solution.py:286
  699.3 380.1 %copy-start.5 = (s32[128]{0:T(128)S(1)}, s32[128]{0:T(128)}, u32[]{:S(2)}) copy-start(s32[128]{0:T(128)} %copy-done.4) | copy-start | bytes 1540
  699.3 380.2 %copy-start.1 = (bf16[256,1440]{1,0:T(8,128)(2,1)S(1)}, bf16[256,1440]{1,0:T(8,128)(2,1)}, u32[]{:S(2)}) copy-start(bf16[256,1440]{1,0:T(8,128)(2,1)} %table.3.table_ref) | copy-start | bytes 2211844
  1074.6 4.9 copy-start
  1074.6 64.7 %all-to-all-start.4 = ((bf16[16,24,24,128]{3,2,1,0:T(8,128)(2,1)}), bf16[16,24,24,128]{3,2,1,0:T(8,128)(2,1)}, u32[]{:S(2)}, u32[]{:S(2)}) async-start(bf16[16,24,24,128]{3,2,1,0:T(8,128)(2,1)} %slice.35), calls=%async_computation.4 | async-start | bytes 4718592 | tf_op jit(solution)/shard_map/all_to_all | solution.py:297

commit v3 on v2

--- a/solution.py
+++ b/solution.py
@@ -266,19 +266,27 @@
         tables.append(build_table(orders, lon_count))
         weights += [jnp.where(orders == 0, 1.0, 2.0)] * 2
         sent = analyse(state, tables[-1], targets, size, wide_tile)
-        if arrived:
-            sent, arrived[-1] = lax.optimization_barrier((sent, arrived[-1]))
-        arrived.append(exchange(sent))
+        arrived.append(sent)
         first += size
 
-    backs = []
-    first = 0
-    for size, got in zip(sizes, arrived):
+    def there_and_back(got, size, first):
         got = got.reshape(lat_count, ord_count, lat_rows, size, 2 * channels)
         got = got.transpose(3, 1, 0, 2, 4)
         done = legendre_stage(got, legendre, mine[first : first + size], gain, mix, first)
-        backs.append(done.transpose(2, 1, 3, 0, 4).reshape(targets, lat_rows, size, 2 * channels))
-        first += size
+        return done.transpose(2, 1, 3, 0, 4).reshape(targets, lat_rows, size, 2 * channels)
+
+    got = exchange(arrived[0])
+    if len(sizes) == 1:
+        backs = [there_and_back(got, sizes[0], 0)]
+    else:
+        head = wide_tile
+        ahead, behind = arrived[1][:, :head], arrived[1][:, head:]
+        ahead, behind, got = lax.optimization_barrier((ahead, behind, got))
+        ahead = exchange(ahead)
+        backs = [there_and_back(got, sizes[0], 0)]
+        behind, ahead, backs[0] = lax.optimization_barrier((behind, ahead, backs[0]))
+        got = jnp.concatenate([ahead, exchange(behind)], axis=1)
+        backs.append(there_and_back(got, sizes[1], sizes[0]))
     inverse = (
         jnp.concatenate(tables, axis=0) * jnp.concatenate(weights)[:, None]
     ).astype(jnp.bfloat16)

time: 1150 us -> 1140 us (level)
  waiting for transfers between devices: 496 us -> 114 us
  blocking collectives: 339 us -> 686 us
    all_to_all x2, waiting for transfers between devices: 459 us -> 81.5 us  [the longest x1 81.5 us: shards(): got = exchange(arrived[0])]
    all_to_all x0 -> x1, blocking collectives: none -> 347 us  [shards(): got = jnp.concatenate([ahead, exchange(behind)], axis=1)]
    slice x2 -> x4, local copies, waits for them, and re-layouts: 1.2 us -> 18.3 us  [the longest x2 17.1 us: shards(): ahead, behind = (arrived[1][:, :head], arrived[1][:, head:])]
  transfers between devices with their start and end apart: 4 -> 4, of which waited for: 3 -> 2; matrix products, arithmetic and copies ran while one was open for 5% -> 7% of each run, Pallas kernels for 17% -> 18%
where the time goes in v3:
time: 1140 us
  blocking collectives  686 us (60%)
  Pallas kernels  236 us (21%)
  waiting for transfers between devices  114 us (10%)
  local copies, waits for them, and re-layouts  67.2 us (6%)
  starting transfers between devices  22.7 us (2%)
  other arithmetic  15.3 us (1%)
    all_to_all x1, blocking collectives, shards(): got = jnp.concatenate([ahead, exchange(behind)], axis=1)  347 us
    all_to_all x1, blocking collectives, shards(): early = exchange(early)  339 us
    pallas_call x2, Pallas kernels, legendre_stage(): pl.pallas_call(functools.partial(legendre_kernel, part=part), grid_spec=p...  106 us
    all_to_all x1, waiting for transfers between devices, shards(): got = exchange(arrived[0])  81.5 us
    pallas_call x2, Pallas kernels, synthesise(): pl.pallas_call(functools.partial(synthesis_kernel, count=len(chunks), gro...  70.1 us
    pallas_call x2, Pallas kernels, analyse(): pl.pallas_call(functools.partial(analysis_kernel, group=group), grid=(lat...  53.9 us
    all_to_all x1, waiting for transfers between devices, shards(): settled = [exchange(back) for back in backs[:-1]]  32.3 us
  transfers between devices with their start and end apart: 4, of which 2 were waited for; matrix products, arithmetic and copies ran while one was open for 7% of the time, Pallas kernels for 18%

profile of v3, /device:TPU:0, one launch (start us, length us, event | category | flops | bytes accessed | tf_op | source)
XLA Modules:
  0.0 1141.8 jit_solution(8536630347878275178)
XLA Ops:
  0.0 0.8 reshape.70
  0.8 0.1 mul.84
  0.9 0.0 copy-start.6
  0.9 1.3 fusion.11
  2.2 2.4 table.3.table_ref
  4.6 19.6 %analysis.3 = bf16[16,180,8,128]{3,2,1,0:T(8,128)(2,1)} custom-call(bf16[180,64,1440]{2,1,0:T(8,128)(2,1)} %bitcast.21, bf16[256,1440]{1,0:T(8,128)(2,1)} %table.3.table_ref), custom_call_target="tpu_custom_call" | custom-call | flops 8493465600 | bytes 39075840 | tf_op jit(solution)/shard_map/analysis/pallas_call | solution.py:75
  24.2 0.0 copy-done.6
  24.2 8.4 all-to-all-start
  32.5 0.1 slice.40
  32.6 0.1 mul.77
  32.7 0.0 copy-start.4
  32.7 2.7 fusion.4
  35.4 4.0 table.2.table_ref
  39.4 34.3 %analysis.2 = bf16[16,180,24,128]{3,2,1,0:T(8,128)(2,1)} custom-call(bf16[180,64,1440]{2,1,0:T(8,128)(2,1)} %bitcast.22, bf16[768,1440]{1,0:T(8,128)(2,1)} %table.2.table_ref), custom_call_target="tpu_custom_call" | custom-call | flops 25480396800 | bytes 50872320 | tf_op jit(solution)/shard_map/analysis/pallas_call | solution.py:75
  73.7 3.2 slice.41
  76.8 13.9 %slice.42 = bf16[16,160,24,128]{3,2,1,0:T(8,128)(2,1)} slice(bf16[16,180,24,128]{3,2,1,0:T(8,128)(2,1)} %analysis.2), slice={[0:16], [20:180], [0:24], [0:128]} | slice | bytes 31457280 | tf_op jit(solution)/shard_map/slice | solution.py:283
  90.8 81.5 %all-to-all-done = bf16[16,180,8,128]{3,2,1,0:T(8,128)(2,1)} async-done(((bf16[16,180,8,128]{3,2,1,0:T(8,128)(2,1)}), bf16[16,180,8,128]{3,2,1,0:T(8,128)(2,1)}, u32[]{:S(2)}, u32[]{:S(2)}) %all-to-all-start) | async-done | bytes 5898272 | tf_op jit(solution)/shard_map/all_to_all | solution.py:278
  172.2 4.6 all-to-all-start.1
  176.9 0.0 copy-done.3
  176.9 0.2 mul.90
  177.1 0.9 broadcast_multiply_fusion
  178.0 1.4 mul.94.mix_ref
  179.4 0.3 copy.10
  179.7 0.2 concatenate.22
  179.9 0.5 broadcast_in_dim.28
  180.4 2.3 copy.11.gain_ref
  182.7 0.6 slice_bitcast_fusion.order_ref
  183.3 6.3 copy.19
  189.6 29.7 %legendre.2 = bf16[8,4,4,180,128]{4,3,2,1,0:T(8,128)(2,1)} custom-call(s32[8]{0:T(128)} %slice_bitcast_fusion.order_ref, bf16[8,4,4,180,128]{4,3,2,1,0:T(8,128)(2,1)} %bitcast.28, bf16[32,720,720]{2,1,0:T(8,128)(2,1)} %leg_ref.3, f32[1448,512]{1,0:T(8,128)} %copy.11.gain_ref, bf16[512,512]{1,0:T(8,128)(2,1)} %mul.94.mix_ref), custom_call_target="tpu_custom_call" | custom-call | flops 11513364480 | bytes 20090880 | tf_op jit(solution)/shard_map/legendre/pallas_call | solution.py:137
  219.3 9.0 copy.12
  228.3 0.0 all-to-all-done.1
  228.3 347.4 %all_to_all.30 = bf16[16,160,24,128]{3,2,1,0:T(8,128)(2,1)} all-to-all(bf16[16,160,24,128]{3,2,1,0:T(8,128)(2,1)} %slice.42), channel_id=1, replica_groups=mesh['lat'=4,'ord'=4,'batch'=2] {'lat','ord'}, dimensions={0} | all-to-all | bytes 31457280 | tf_op jit(solution)/shard_map/all_to_all | solution.py:288
  575.7 4.8 all-to-all-start.3
  580.5 0.6 slice_bitcast_fusion.1.order_ref
  581.1 8.1 pad_maximum_fusion
  589.2 8.6 copy.18
  597.8 76.2 %legendre.3 = bf16[24,4,4,180,128]{4,3,2,1,0:T(8,128)(2,1)} custom-call(s32[24]{0:T(128)} %slice_bitcast_fusion.1.order_ref, bf16[24,4,4,180,128]{4,3,2,1,0:T(8,128)(2,1)} %bitcast.31, bf16[32,720,720]{2,1,0:T(8,128)(2,1)} %leg_ref.3, f32[1448,512]{1,0:T(8,128)} %copy.11.gain_ref, bf16[512,512]{1,0:T(8,128)(2,1)} %mul.94.mix_ref), custom_call_target="tpu_custom_call" | custom-call | flops 34540093440 | bytes 60272640 | tf_op jit(solution)/shard_map/legendre/pallas_call | solution.py:137
  674.0 11.4 copy.15
  685.4 2.0 slice.45
  687.4 5.8 slice.44
  693.2 32.3 %all-to-all-done.3.refs_0_ = bf16[16,180,8,128]{3,2,1,0:T(8,128)(2,1)} async-done(((bf16[16,180,8,128]{3,2,1,0:T(8,128)(2,1)}), bf16[16,180,8,128]{3,2,1,0:T(8,128)(2,1)}, u32[]{:S(2)}, u32[]{:S(2)}) %all-to-all-start.3) | async-done | bytes 5898272 | tf_op jit(solution)/shard_map/all_to_all | solution.py:294
  725.5 339.0 %all_to_all.31.refs_1_ = bf16[16,156,24,128]{3,2,1,0:T(8,128)(2,1)} all-to-all(bf16[16,156,24,128]{3,2,1,0:T(8,128)(2,1)} %slice.44), channel_id=1, replica_groups=mesh['lat'=4,'ord'=4,'batch'=2] {'lat','ord'}, dimensions={0} | all-to-all | bytes 30670848 | tf_op jit(solution)/shard_map/all_to_all | solution.py:303
  1064.5 4.8 all-to-all-start.5
  1069.3 0.0 copy-done.7
  1069.4 2.2 maximum_multiply_fusion.refs_2_
  1071.6 57.5 %synthesis.2.refs_4_ = bf16[180,64,1440]{2,1,0:T(8,128)(2,1)} custom-call(bf16[16,180,8,128]{3,2,1,0:T(8,128)(2,1)} %all-to-all-done.3.refs_0_, bf16[16,156,24,128]{3,2,1,0:T(8,128)(2,1)} %all_to_all.31.refs_1_, bf16[1024,1440]{1,0:T(8,128)(2,1)} %maximum_multiply_fusion.refs_2_, bf16[180,64,1440]{2,1,0:T(8,128)(2,1)} %bitcast.23), custom_call_target="tpu_custom_call" | custom-call | flops 29444014080 | bytes 77955072 | tf_op jit(solution)/shard_map/synthesis/pallas_call | solution.py:213
  1129.1 0.0 all-to-all-done.5.refs_1_
  1129.1 12.7 %synthesis.3 = bf16[180,64,1440]{2,1,0:T(8,128)(2,1)} custom-call(bf16[16,180,8,128]{3,2,1,0:T(8,128)(2,1)} %all-to-all-done.3.refs_0_, bf16[16,24,24,128]{3,2,1,0:T(8,128)(2,1)} %all-to-all-done.5.refs_1_, bf16[1024,1440]{1,0:T(8,128)(2,1)} %maximum_multiply_fusion.refs_2_, bf16[180,64,1440]{2,1,0:T(8,128)(2,1)} %bitcast.24, ...), custom_call_target="tpu_custom_call", output_to_operand_aliasing={{}: (4, {})} | custom-call | flops 4529848320 | bytes 11993088 | tf_op jit(solution)/shard_map/synthesis/pallas_call | solution.py:213
  (19 shorter events, 0.1 us)
Async XLA Ops:
  0.9 23.3 %copy-start.6 = (s32[128]{0:T(128)}, s32[128]{0:T(128)S(1)}, u32[]{:S(2)}) copy-start(s32[128]{0:T(128)S(1)} %mul.84) | copy-start | bytes 1540
  24.2 148.1 %all-to-all-start = ((bf16[16,180,8,128]{3,2,1,0:T(8,128)(2,1)}), bf16[16,180,8,128]{3,2,1,0:T(8,128)(2,1)}, u32[]{:S(2)}, u32[]{:S(2)}) async-start(bf16[16,180,8,128]{3,2,1,0:T(8,128)(2,1)} %analysis.3), calls=%async_computation | async-start | bytes 11796480 | tf_op jit(solution)/shard_map/all_to_all | solution.py:278
  32.7 40.9 %copy-start.4 = (s32[384]{0:T(512)}, s32[384]{0:T(512)S(1)}, u32[]{:S(2)}) copy-start(s32[384]{0:T(512)S(1)} %mul.77) | copy-start | bytes 4612
  76.8 100.0 %copy-start.3 = (bf16[256,256]{1,0:T(8,128)(2,1)S(1)}, bf16[256,256]{1,0:T(8,128)(2,1)}, u32[]{:S(2)}) copy-start(bf16[256,256]{1,0:T(8,128)(2,1)} %param.9) | copy-start | bytes 393220
  90.7 88.7 %copy-start.2 = (f32[720,256]{1,0:T(8,128)S(1)}, f32[720,256]{1,0:T(8,128)}, u32[]{:S(2)}) copy-start(f32[720,256]{1,0:T(8,128)} %param.8) | copy-start | bytes 2211844
  172.2 56.0 %all-to-all-start.1 = ((bf16[16,20,24,128]{3,2,1,0:T(8,128)(2,1)}), bf16[16,20,24,128]{3,2,1,0:T(8,128)(2,1)}, u32[]{:S(2)}, u32[]{:S(2)}) async-start(bf16[16,20,24,128]{3,2,1,0:T(8,128)(2,1)} %slice.41), calls=%async_computation.1 | async-start | bytes 3932160 | tf_op jit(solution)/shard_map/all_to_all | solution.py:285
  575.7 149.8 %all-to-all-start.3 = ((bf16[16,180,8,128]{3,2,1,0:T(8,128)(2,1)}), bf16[16,180,8,128]{3,2,1,0:T(8,128)(2,1)}, u32[]{:S(2)}, u32[]{:S(2)}) async-start(bf16[16,180,8,128]{3,2,1,0:T(8,128)(2,1)} %bitcast.30), calls=%async_computation.3 | async-start | bytes 11796480 | tf_op jit(solution)/shard_map/all_to_all | solution.py:294
  693.2 376.1 %copy-start.7 = (s32[128]{0:T(128)S(1)}, s32[128]{0:T(128)}, u32[]{:S(2)}) copy-start(s32[128]{0:T(128)} %copy-done.6) | copy-start | bytes 1540
  693.2 376.1 %copy-start.5 = (s32[384]{0:T(512)S(1)}, s32[384]{0:T(512)}, u32[]{:S(2)}) copy-start(s32[384]{0:T(512)} %copy-done.4) | copy-start | bytes 4612
  693.2 376.2 %copy-start.1 = (bf16[256,1440]{1,0:T(8,128)(2,1)S(1)}, bf16[256,1440]{1,0:T(8,128)(2,1)}, u32[]{:S(2)}) copy-start(bf16[256,1440]{1,0:T(8,128)(2,1)} %table.3.table_ref) | copy-start | bytes 2211844
  1064.5 4.9 copy-start
  1064.5 64.6 %all-to-all-start.5 = ((bf16[16,24,24,128]{3,2,1,0:T(8,128)(2,1)}), bf16[16,24,24,128]{3,2,1,0:T(8,128)(2,1)}, u32[]{:S(2)}, u32[]{:S(2)}) async-start(bf16[16,24,24,128]{3,2,1,0:T(8,128)(2,1)} %slice.45), calls=%async_computation.5 | async-start | bytes 4718592 | tf_op jit(solution)/shard_map/all_to_all | solution.py:305
